TPU v7x, 32 devices: a whole 2x2x4 slice. The times are simulated.
32 devices in a mesh: lat: 16 (over z, y, x), fld: 2 (over core).
Axes of the slice: x: 2, y: 2, z: 4, core: 2. Of those that a mesh axis runs over, the one named last changes fastest.
Arguments:
- grid: bfloat16 [2, 4, 69, 640, 1408], P('fld', None, None, 'lat'), may hold values from -6 to 6
- cycle_ids: int32 [640], replicated, may hold values from 0 to 639, each once
- cycle_len: int32 [640], replicated, may hold values from 20 to 1296, as said below
- wave_ids: int32 [320], replicated, may hold values from 0 to 319, each once
- legendre: bfloat16 [320, 320, 640], P('lat'), may hold values from -0.25 to 0.25
- target: float32 [2, 4, 69, 2, 320, 320], P('fld', None, None, None, 'lat'), may hold values from -18 to 18
- step_w: float32 [2], P('fld'), may hold values from 0.5 to 2
- chan_w: float32 [69], replicated, may hold values from 0.2 to 2
Outputs:
- coeffs: float32 [2, 4, 69, 2, 320, 320], P('fld', None, None, None, 'lat')
- loss: float32 [], replicated
- field_grad: bfloat16 [2, 4, 69, 640, 1408], P('fld', None, None, 'lat')
Inputs may be any that keep to these rules, and one draw needn't show every extreme that they name: `cycle_len`: every length 20 + 4 j with j from 0 to 319 occurs exactly twice.
All inputs are finite; a program needn't handle non-finite values.
Results may differ from a plain program's by a relative error of at most 0.0065.
Values may be sent and summed in bfloat16 or wider, within the bound.
No kernel may reach another device: no remote copies, remote signals or barrier semaphores. Data moves between devices by JAX's collectives and lax.ppermute only.
A program may use at most 320 MiB of HBM per device.

v0:
```python
import math
import jax
import jax.numpy as jnp
from jax import lax
from jax.sharding import PartitionSpec as P

STEPS = 2


def cycle_table(length, wave_order, segment):
    slot_index = jnp.arange(segment, dtype=jnp.int32)
    phase_int = slot_index[:, None] * wave_order[None, :] % length
    angles = 2.0 * math.pi / length.astype(jnp.float32) * phase_int.astype(jnp.float32)
    inside = (slot_index[:, None] < length) & (2 * wave_order[None, :] < length)
    row_scale = jnp.where(inside, lax.rsqrt(length.astype(jnp.float32)), jnp.float32(0.0))
    paired = jnp.stack([jnp.cos(angles) * row_scale, -jnp.sin(angles) * row_scale], axis=2)
    return paired.reshape(segment, 2 * wave_order.shape[0]).astype(jnp.bfloat16)


def owner_pass(
    part_fourier, legendre_cols, kept_mask, factor, target_part, weight_part, send_out, send_back
):
    gathered = send_out(part_fourier)
    coeffs = jnp.einsum(
        "jnr,rbjp->jnbp", legendre_cols, gathered, preferred_element_type=jnp.float32
    )
    coeffs = coeffs * kept_mask
    weight = factor[:, None, None, None] * weight_part[None, None, :, None]
    misfit = (coeffs - target_part) * kept_mask
    partial_value = jnp.sum(weight * misfit * misfit)
    grad_coeff = (2.0 * weight * misfit).astype(jnp.bfloat16)
    back_rows = jnp.einsum(
        "jnr,jnbp->rbjp", legendre_cols, grad_coeff, preferred_element_type=jnp.float32
    )
    back_rows = back_rows.astype(jnp.bfloat16)
    returned = send_back(back_rows)
    return (coeffs, partial_value, returned)


def per_device(grid, cycle_ids, cycle_len, wave_ids, legendre, target, step_w, chan_w):
    batch_size, chan_count, cycle_dev, segment = (
        grid.shape[1],
        grid.shape[2],
        grid.shape[3],
        grid.shape[4],
    )
    wave_count = wave_ids.shape[0]
    wave_dev = legendre.shape[0]
    col_count = batch_size * chan_count
    lat_index = lax.axis_index("lat")
    my_cycles = lax.dynamic_slice_in_dim(cycle_ids, lat_index * cycle_dev, cycle_dev)
    lengths = jnp.take(cycle_len, my_cycles)
    tables = jax.vmap(lambda length: cycle_table(length, wave_ids, segment))(lengths)
    fourier = jnp.einsum("bcrk,rkj->rbcj", grid[0], tables, preferred_element_type=jnp.float32)
    fourier = fourier.astype(jnp.bfloat16).reshape(cycle_dev, col_count, wave_count, 2)
    my_waves = lax.dynamic_slice_in_dim(wave_ids, lat_index * wave_dev, wave_dev)
    legendre_cols = jnp.take(legendre, cycle_ids, axis=2)
    degree = jnp.arange(wave_count, dtype=jnp.int32)
    kept_mask = (degree[None, :] >= my_waves[:, None]).astype(jnp.float32)[:, :, None, None]
    target_local = jnp.transpose(
        target[0].reshape(col_count, 2, wave_dev, wave_count), (2, 3, 0, 1)
    )
    factor = jnp.where(my_waves == 0, 1.0, 2.0).astype(jnp.float32)
    weight_cols = jnp.broadcast_to(step_w[0] * chan_w[None, :], (batch_size, chan_count)).reshape(
        col_count
    )

    def send_out(values):
        return lax.all_to_all(values, "lat", split_axis=2, concat_axis=0, tiled=True)

    def send_back(values):
        return lax.all_to_all(values, "lat", split_axis=0, concat_axis=2, tiled=True)

    coeff_piece, partial_piece, returned_piece = owner_pass(
        fourier, legendre_cols, kept_mask, factor, target_local, weight_cols, send_out, send_back
    )
    returned = returned_piece
    returned = returned.reshape(cycle_dev, col_count, 2 * wave_count)
    field_rows = jnp.einsum("rbj,rkj->brk", returned, tables, preferred_element_type=jnp.float32)
    field_grad = field_rows.astype(jnp.bfloat16).reshape(
        1, batch_size, chan_count, cycle_dev, segment
    )
    coeff_out = jnp.transpose(coeff_piece, (2, 3, 0, 1)).reshape(
        1, batch_size, chan_count, 2, wave_dev, wave_count
    )
    loss_sum = lax.psum(partial_piece, ("lat", "fld"))
    term_count = STEPS * batch_size * chan_count * wave_count * (wave_count + 1) // 2
    loss = loss_sum / jnp.float32(term_count)
    return (coeff_out, loss, field_grad)


def solution(mesh):
    return jax.shard_map(
        per_device,
        mesh=mesh,
        in_specs=(
            P("fld", None, None, "lat", None),
            P(),
            P(),
            P(),
            P("lat", None, None),
            P("fld", None, None, None, "lat", None),
            P("fld"),
            P(),
        ),
        out_specs=(P("fld", None, None, None, "lat", None), P(), P("fld", None, None, "lat", None)),
        check_vma=False,
    )
```

profile of v0, /device:TPU:0, one launch (start us, length us, event | category | flops | bytes accessed | tf_op | source)
XLA Modules:
  0.0 2604.8 jit_solution(16800594429964141860)
XLA Ops:
  0.6 0.0 copy-start
  0.7 0.8 compare_select_fusion.2
  1.4 0.0 copy-done
  1.4 0.7 gather_fusion.1
  2.2 0.8 broadcast_compare_fusion.1
  2.9 0.1 iota_compare_fusion
  3.1 0.7 broadcast_multiply_fusion.2
  3.7 0.9 iota_multiply_fusion
  4.6 0.1 broadcast_compare_fusion
  4.7 1187.4 %fusion = (bf16[40,1408,320,1]{1,0,3,2:T(8,128)(2,1)}, bf16[40,1408,320,1]{1,0,3,2:T(8,128)(2,1)}) fusion(f32[40]{0:T(128)S(1)} %get-tuple-element.17, s32[40]{0:T(128)S(1)} %compare_select_fusion.1, s32[1408,320]{0,1:T(8,128)S(1)} %iota_multiply_fusion, f32[40]{0:T(128)S(1)} %get-tuple-element.16, pred[40]{0:T(512)(128)(4,1)S(1)} %get-tuple-element.8, ...), kind=kLoop, calls=%fused_computation.8 | loop fusion | flops 288358400 | bytes 73961480 | tf_op jit(solution)/shard_map/convert
  1192.1 48.1 %pad_maximum_fusion = bf16[40,1408,320,2]{1,0,3,2:T(8,128)(2,1)} fusion(bf16[40,1408,320,1]{1,0,3,2:T(8,128)(2,1)} %get-tuple-element.13, bf16[40,1408,320,1]{1,0,3,2:T(8,128)(2,1)} %get-tuple-element.12), kind=kLoop, calls=%fused_computation.15 | loop fusion | flops 36044800 | bytes 144179200 | tf_op jit(solution)/shard_map/vmap()/stack | solution.py:16
  1240.2 88.0 %convert_bitcast_fusion.1 = bf16[40,4,69,640]{3,2,1,0:T(8,128)(2,1)} fusion(bf16[4,69,40,1408]{3,2,1,0:T(8,128)(2,1)} %bitcast.51, bf16[40,1408,640,1]{1,0,2,3:T(8,128)(2,1)} %bitcast.3), kind=kOutput, calls=%fused_computation.31 | convolution fusion | flops 19903795200 | bytes 117309440 | tf_op jit(solution)/shard_map/bcrk,rkj->rbcj/dot_general | solution.py:54
  1328.2 41.0 %copy.35 = bf16[40,4,69,640]{2,1,0,3:T(4,128)(2,1)} copy(bf16[40,4,69,640]{3,2,1,0:T(8,128)(2,1)} %convert_bitcast_fusion.1) | data formatting | bytes 28262400 | tf_op jit(solution)/shard_map/convert_element_type | solution.py:55
  1369.2 40.3 %reshape.263 = bf16[40,276,320,2]{1,0,3,2:T(8,128)(2,1)} reshape(bf16[40,4,69,640]{2,1,0,3:T(4,128)(2,1)} %copy.35) | data formatting | bytes 28262400 | tf_op jit(solution)/shard_map/reshape | solution.py:55
  1409.6 8.6 all-to-all-start
  1418.2 0.0 copy-start.3
  1418.2 15.0 copy.32
  1433.2 0.0 copy-done.3
  1433.2 25.5 gather_fusion
  1458.7 0.0 copy-start.4
  1458.7 11.0 select_bitcast_fusion
  1469.8 14.9 copy.49
  1485.3 0.0 copy-done.4
  1485.3 0.1 mul.164
  1485.4 0.8 compare_select_fusion.3
  1486.1 0.1 fusion.25
  1486.2 0.1 broadcast_multiply_fusion
  1486.3 300.9 %all-to-all-done = bf16[40,276,320,2]{1,0,3,2:T(8,128)(2,1)} async-done(((bf16[40,276,320,2]{1,0,3,2:T(8,128)(2,1)}), bf16[40,276,320,2]{1,0,3,2:T(8,128)(2,1)}, u32[]{:S(2)}, u32[]{:S(2)}) %all-to-all-start) | async-done | bytes 14131232 | tf_op jit(solution)/shard_map/all_to_all | solution.py:69
  1787.2 0.0 copy-start.2
  1787.2 17.2 copy.36
  1804.4 0.0 copy-done.2
  1804.4 18.7 fusion.26
  1823.1 23.4 convert_bitcast_fusion.2
  1846.5 47.3 %copy.42 = bf16[640,276,20,2]{1,3,2,0:T(2,128)(2,1)} copy(bf16[640,276,20,2]{0,1,3,2:T(8,128)(2,1)} %convert_bitcast_fusion.2) | data formatting | bytes 28262400 | tf_op jit(solution)/shard_map/convert_element_type | solution.py:35
  1893.7 86.3 %all-to-all-start.1 = ((bf16[640,276,20,2]{1,3,2,0:T(2,128)(2,1)}), bf16[640,276,20,2]{1,3,2,0:T(2,128)(2,1)}, u32[]{:S(2)}, u32[]{:S(2)}) async-start(bf16[640,276,20,2]{1,3,2,0:T(2,128)(2,1)} %copy.42), calls=%async_computation.1 | async-start | bytes 39321600 | tf_op jit(solution)/shard_map/all_to_all | solution.py:72
  1980.0 19.0 fusion.17
  1999.0 447.4 %psum.7 = f32[]{:T(128)} all-reduce(f32[]{:T(128)} %get-tuple-element.10), channel_id=1, replica_groups=mesh['lat'=16,'fld'=2] {'lat','fld'}, use_global_device_ids=true, to_apply=%region_1.2 | all-reduce | flops 1 | bytes 8 | tf_op jit(solution)/shard_map/psum | solution.py:86
  2446.4 30.0 %copy.39 = f32[276,2,20,320]{3,1,2,0:T(2,128)} copy(f32[276,2,20,320]{3,0,1,2:T(8,128)} %get-tuple-element.11) | data formatting | bytes 28262400 | tf_op jit(solution)/shard_map/mul | solution.py:27
  2477.0 0.0 all-to-all-done.1
  2477.0 11.8 copy.43
  2488.9 7.0 copy.44
  2495.9 0.0 copy-start.1
  2495.9 72.0 %convert_bitcast_fusion = bf16[276,40,1408]{2,0,1:T(8,128)(2,1)} fusion(bf16[40,1408,640]{1,0,2:T(8,128)(2,1)} %bitcast.2, bf16[40,276,640]{1,0,2:T(8,128)(2,1)} %bitcast.49), kind=kOutput, calls=%fused_computation.23 | convolution fusion | flops 19912273920 | bytes 117309440 | tf_op jit(solution)/shard_map/rbj,rkj->brk/dot_general | solution.py:79
  2567.9 35.6 %copy.47 = bf16[276,40,1408]{2,1,0:T(8,128)(2,1)} copy(bf16[276,40,1408]{2,0,1:T(8,128)(2,1)} %convert_bitcast_fusion) | data formatting | bytes 62177280 | tf_op jit(solution)/shard_map/convert_element_type | solution.py:80
  2603.5 0.0 copy-done.1
  (8 shorter events, 0.0 us)
Async XLA Ops:
  0.6 0.8 copy-start
  1409.6 377.6 %all-to-all-start = ((bf16[40,276,320,2]{1,0,3,2:T(8,128)(2,1)}), bf16[40,276,320,2]{1,0,3,2:T(8,128)(2,1)}, u32[]{:S(2)}, u32[]{:S(2)}) async-start(bf16[40,276,320,2]{1,0,3,2:T(8,128)(2,1)} %reshape.263), calls=%async_computation | async-start | bytes 39321600 | tf_op jit(solution)/shard_map/all_to_all | solution.py:69
  1418.2 15.0 copy-start.3
  1458.7 26.5 %copy-start.4 = (f32[69]{0:T(128)S(1)}, f32[69]{0:T(128)}, u32[]{:S(2)}) copy-start(f32[69]{0:T(128)} %param.15) | copy-start | bytes 832
  1787.2 17.2 copy-start.2
  1893.7 583.3 %all-to-all-start.1 = ((bf16[640,276,20,2]{1,3,2,0:T(2,128)(2,1)}), bf16[640,276,20,2]{1,3,2,0:T(2,128)(2,1)}, u32[]{:S(2)}, u32[]{:S(2)}) async-start(bf16[640,276,20,2]{1,3,2,0:T(2,128)(2,1)} %copy.42), calls=%async_computation.1 | async-start | bytes 39321600 | tf_op jit(solution)/shard_map/all_to_all | solution.py:72
  2495.9 107.6 %copy-start.1 = (s32[640]{0:T(1024)S(1)}, s32[640]{0:T(1024)}, u32[]{:S(2)}) copy-start(s32[640]{0:T(1024)} %param.10) | copy-start | bytes 7684
where the time goes:
time: 2610 us; the launch traced here: 2600 us
  other arithmetic  1270 us (49%)
  blocking collectives  447 us (17%)
  waiting for transfers between devices  301 us (12%)
  local copies, waits for them, and re-layouts  287 us (11%)
  matrix products  202 us (8%)
  starting transfers between devices  94.9 us (4%)
    another operation x1, other arithmetic  1190 us
    psum x1, blocking collectives, per_device(): loss_sum = lax.psum(partial_piece, ('lat', 'fld'))  447 us
    all_to_all x1, waiting for transfers between devices, send_out(): lax.all_to_all(values, 'lat', split_axis=2, concat_axis=0, tiled=True)  301 us
    dot_general x1, matrix products, per_device(): jnp.einsum('bcrk,rkj->rbcj', grid[0], tables, preferred_element_type=jnp....  88 us
    all_to_all x1, starting transfers between devices, send_back(): lax.all_to_all(values, 'lat', split_axis=0, concat_axis=2, tiled=True)  86.3 us
    dot_general x1, matrix products, per_device(): jnp.einsum('rbj,rkj->brk', returned, tables, preferred_element_type=jnp.f...  72 us
  transfers between devices with their start and end apart: 2, of which 1 were waited for; matrix products, arithmetic and copies ran while one was open for 4% of the time, Pallas kernels for 0%

commit v1 on v0

--- a/solution.py
+++ b/solution.py
@@ -83,7 +83,8 @@
     coeff_out = jnp.transpose(coeff_piece, (2, 3, 0, 1)).reshape(
         1, batch_size, chan_count, 2, wave_dev, wave_count
     )
-    loss_sum = lax.psum(partial_piece, ("lat", "fld"))
+    parts = lax.all_gather(partial_piece, ("lat", "fld"), axis=0, tiled=False)
+    loss_sum = parts.sum(axis=0)
     term_count = STEPS * batch_size * chan_count * wave_count * (wave_count + 1) // 2
     loss = loss_sum / jnp.float32(term_count)
     return (coeff_out, loss, field_grad)

time: 2610 us -> 2610 us (level)
    psum x1 -> x0, blocking collectives: 447 us -> none  [per_device(): loss_sum = lax.psum(partial_piece, ('lat', 'fld'))]
    unnamed x0 -> x1, blocking collectives: none -> 447 us
  transfers between devices with their start and end apart: 2 -> 2, of which waited for: 1 -> 1; matrix products, arithmetic and copies ran while one was open for 4% -> 5% of each run, Pallas kernels for 0% -> 0%
where the time goes in v1:
time: 2610 us
  other arithmetic  1270 us (49%)
  blocking collectives  447 us (17%)
  waiting for transfers between devices  301 us (12%)
  local copies, waits for them, and re-layouts  287 us (11%)
  matrix products  202 us (8%)
  starting transfers between devices  94.9 us (4%)
    another operation x1, other arithmetic  1190 us
    unnamed x1, blocking collectives  447 us
    all_to_all x1, waiting for transfers between devices, send_out(): lax.all_to_all(values, 'lat', split_axis=2, concat_axis=0, tiled=True)  301 us
    dot_general x1, matrix products, per_device(): jnp.einsum('bcrk,rkj->rbcj', grid[0], tables, preferred_element_type=jnp....  88 us
    all_to_all x1, starting transfers between devices, send_back(): lax.all_to_all(values, 'lat', split_axis=0, concat_axis=2, tiled=True)  86.3 us
    dot_general x1, matrix products, per_device(): jnp.einsum('rbj,rkj->brk', returned, tables, preferred_element_type=jnp.f...  72 us
  transfers between devices with their start and end apart: 2, of which 1 were waited for; matrix products, arithmetic and copies ran while one was open for 5% of the time, Pallas kernels for 0%

profile of v1, /device:TPU:0, one launch (start us, length us, event | category | flops | bytes accessed | tf_op | source)
XLA Modules:
  0.0 2605.4 jit_solution(344248687325156076)
XLA Ops:
  0.6 0.0 copy-start
  0.7 0.8 compare_select_fusion.2
  1.4 0.0 copy-done
  1.4 0.7 gather_fusion.1
  2.2 0.8 broadcast_compare_fusion.1
  2.9 0.1 iota_compare_fusion
  3.1 0.7 broadcast_multiply_fusion.2
  3.7 0.9 iota_multiply_fusion
  4.6 0.1 broadcast_compare_fusion
  4.7 1187.4 %fusion = (bf16[40,1408,320,1]{1,0,3,2:T(8,128)(2,1)}, bf16[40,1408,320,1]{1,0,3,2:T(8,128)(2,1)}) fusion(f32[40]{0:T(128)S(1)} %get-tuple-element.17, s32[40]{0:T(128)S(1)} %compare_select_fusion.1, s32[1408,320]{0,1:T(8,128)S(1)} %iota_multiply_fusion, f32[40]{0:T(128)S(1)} %get-tuple-element.16, pred[40]{0:T(512)(128)(4,1)S(1)} %get-tuple-element.8, ...), kind=kLoop, calls=%fused_computation.8 | loop fusion | flops 288358400 | bytes 73961480 | tf_op jit(solution)/shard_map/convert
  1192.1 48.0 %pad_maximum_fusion = bf16[40,1408,320,2]{1,0,3,2:T(8,128)(2,1)} fusion(bf16[40,1408,320,1]{1,0,3,2:T(8,128)(2,1)} %get-tuple-element.13, bf16[40,1408,320,1]{1,0,3,2:T(8,128)(2,1)} %get-tuple-element.12), kind=kLoop, calls=%fused_computation.15 | loop fusion | flops 36044800 | bytes 144179200 | tf_op jit(solution)/shard_map/vmap()/stack | solution.py:16
  1240.2 88.0 %convert_bitcast_fusion.1 = bf16[40,4,69,640]{3,2,1,0:T(8,128)(2,1)} fusion(bf16[4,69,40,1408]{3,2,1,0:T(8,128)(2,1)} %bitcast.52, bf16[40,1408,640,1]{1,0,2,3:T(8,128)(2,1)} %bitcast.3), kind=kOutput, calls=%fused_computation.31 | convolution fusion | flops 19903795200 | bytes 117309440 | tf_op jit(solution)/shard_map/bcrk,rkj->rbcj/dot_general | solution.py:54
  1328.2 41.0 %copy.35 = bf16[40,4,69,640]{2,1,0,3:T(4,128)(2,1)} copy(bf16[40,4,69,640]{3,2,1,0:T(8,128)(2,1)} %convert_bitcast_fusion.1) | data formatting | bytes 28262400 | tf_op jit(solution)/shard_map/convert_element_type | solution.py:55
  1369.2 40.3 %reshape.263 = bf16[40,276,320,2]{1,0,3,2:T(8,128)(2,1)} reshape(bf16[40,4,69,640]{2,1,0,3:T(4,128)(2,1)} %copy.35) | data formatting | bytes 28262400 | tf_op jit(solution)/shard_map/reshape | solution.py:55
  1409.5 8.6 all-to-all-start
  1418.1 0.0 copy-start.3
  1418.1 15.0 copy.32
  1433.1 0.0 copy-done.3
  1433.1 25.5 gather_fusion
  1458.7 0.0 copy-start.4
  1458.7 11.0 select_bitcast_fusion
  1469.7 14.9 copy.49
  1485.2 0.0 copy-done.4
  1485.3 0.1 mul.164
  1485.4 0.8 compare_select_fusion.3
  1486.1 0.1 fusion.25
  1486.2 0.1 broadcast_multiply_fusion
  1486.3 300.9 %all-to-all-done = bf16[40,276,320,2]{1,0,3,2:T(8,128)(2,1)} async-done(((bf16[40,276,320,2]{1,0,3,2:T(8,128)(2,1)}), bf16[40,276,320,2]{1,0,3,2:T(8,128)(2,1)}, u32[]{:S(2)}, u32[]{:S(2)}) %all-to-all-start) | async-done | bytes 14131232 | tf_op jit(solution)/shard_map/all_to_all | solution.py:69
  1787.1 0.0 copy-start.2
  1787.1 17.2 copy.36
  1804.4 0.0 copy-done.2
  1804.4 18.7 fusion.26
  1823.0 23.3 convert_bitcast_fusion.2
  1846.4 47.3 %copy.42 = bf16[640,276,20,2]{1,3,2,0:T(2,128)(2,1)} copy(bf16[640,276,20,2]{0,1,3,2:T(8,128)(2,1)} %convert_bitcast_fusion.2) | data formatting | bytes 28262400 | tf_op jit(solution)/shard_map/convert_element_type | solution.py:35
  1893.7 86.3 %all-to-all-start.1 = ((bf16[640,276,20,2]{1,3,2,0:T(2,128)(2,1)}), bf16[640,276,20,2]{1,3,2,0:T(2,128)(2,1)}, u32[]{:S(2)}, u32[]{:S(2)}) async-start(bf16[640,276,20,2]{1,3,2,0:T(2,128)(2,1)} %copy.42), calls=%async_computation.1 | async-start | bytes 39321600 | tf_op jit(solution)/shard_map/all_to_all | solution.py:72
  1980.0 18.9 fusion.17
  1998.9 0.8 dynamic-update-slice
  1999.7 446.6 %all-reduce = f32[32]{0:T(128)S(1)} all-reduce(f32[32]{0:T(128)S(1)} %dynamic-update-slice), channel_id=1, replica_groups=mesh['lat'=16,'fld'=2] {'lat','fld'}, use_global_device_ids=true, to_apply=%add | all-reduce | flops 32 | bytes 256
  2446.3 30.0 %copy.39 = f32[276,2,20,320]{3,1,2,0:T(2,128)} copy(f32[276,2,20,320]{3,0,1,2:T(8,128)} %get-tuple-element.11) | data formatting | bytes 28262400 | tf_op jit(solution)/shard_map/mul | solution.py:27
  2476.3 0.6 reduce_sum.19
  2477.6 0.0 all-to-all-done.1
  2477.6 11.8 copy.43
  2489.4 7.0 copy.44
  2496.5 0.0 copy-start.1
  2496.5 72.0 %convert_bitcast_fusion = bf16[276,40,1408]{2,0,1:T(8,128)(2,1)} fusion(bf16[40,1408,640]{1,0,2:T(8,128)(2,1)} %bitcast.2, bf16[40,276,640]{1,0,2:T(8,128)(2,1)} %bitcast.50), kind=kOutput, calls=%fused_computation.23 | convolution fusion | flops 19912273920 | bytes 117309440 | tf_op jit(solution)/shard_map/rbj,rkj->brk/dot_general | solution.py:79
  2568.4 35.6 %copy.47 = bf16[276,40,1408]{2,1,0:T(8,128)(2,1)} copy(bf16[276,40,1408]{2,0,1:T(8,128)(2,1)} %convert_bitcast_fusion) | data formatting | bytes 62177280 | tf_op jit(solution)/shard_map/convert_element_type | solution.py:80
  2604.1 0.0 copy-done.1
  (9 shorter events, 0.0 us)
Async XLA Ops:
  0.6 0.8 copy-start
  1409.5 377.6 %all-to-all-start = ((bf16[40,276,320,2]{1,0,3,2:T(8,128)(2,1)}), bf16[40,276,320,2]{1,0,3,2:T(8,128)(2,1)}, u32[]{:S(2)}, u32[]{:S(2)}) async-start(bf16[40,276,320,2]{1,0,3,2:T(8,128)(2,1)} %reshape.263), calls=%async_computation | async-start | bytes 39321600 | tf_op jit(solution)/shard_map/all_to_all | solution.py:69
  1418.1 15.0 copy-start.3
  1458.7 26.6 %copy-start.4 = (f32[69]{0:T(128)S(1)}, f32[69]{0:T(128)}, u32[]{:S(2)}) copy-start(f32[69]{0:T(128)} %param.15) | copy-start | bytes 832
  1787.1 17.2 copy-start.2
  1893.7 583.9 %all-to-all-start.1 = ((bf16[640,276,20,2]{1,3,2,0:T(2,128)(2,1)}), bf16[640,276,20,2]{1,3,2,0:T(2,128)(2,1)}, u32[]{:S(2)}, u32[]{:S(2)}) async-start(bf16[640,276,20,2]{1,3,2,0:T(2,128)(2,1)} %copy.42), calls=%async_computation.1 | async-start | bytes 39321600 | tf_op jit(solution)/shard_map/all_to_all | solution.py:72
  2496.5 107.6 %copy-start.1 = (s32[640]{0:T(1024)S(1)}, s32[640]{0:T(1024)}, u32[]{:S(2)}) copy-start(s32[640]{0:T(1024)} %param.10) | copy-start | bytes 7684
